TPU v7x, 128 devices: a whole 4x4x4 slice. The times are simulated.
128 devices in a mesh: gx: 4 (over z), gy: 8 (over x, core), gz: 4 (over y).
Axes of the slice: x: 4, y: 4, z: 4, core: 2. Of those that a mesh axis runs over, the one named last changes fastest.
Arguments:
- queries: bfloat16 [256, 1024, 512], P(('gx', 'gy'), 'gz'), may hold values from -48 to 48
- key_vectors: bfloat16 [256, 1024, 128], P(('gx', 'gy'), 'gz'), may hold values from -12 to 12
- value_vectors: bfloat16 [256, 1024, 128], P(('gx', 'gy'), 'gz'), may hold values from -6 to 6
- chosen: int32 [256, 2], P(('gx', 'gy')), may hold values from -1 to 255, as said below
Outputs:
- attended: bfloat16 [256, 1024, 512], P(('gx', 'gy'), 'gz')
Inputs may be any that keep to these rules, and one draw needn't show every extreme that they name: `chosen`: both entries of a row are -1, or both are blocks of two different groups before the row's own group, counting blocks in groups of 8 consecutive blocks. One group's rows name blocks of any one group in at most 1 entries; every group from the third on names blocks of the first group in exactly 1 entries. The rows of the first two groups are all -1.
All inputs are finite; a program needn't handle non-finite values.
Results may differ from a plain program's by a relative error of at most 0.0042.
Values may be sent and summed in bfloat16 or wider, within the bound.
A program may use at most 128 MiB of HBM per device.

v0:
```python
import jax
import jax.numpy as jnp
from jax import lax
from jax.sharding import PartitionSpec as P

CAP = 1


def allowed_mask(token_start, query_count, head_count, block_len, live_pair):
    token_pos = token_start + jnp.arange(query_count * head_count, dtype=jnp.int32) // head_count
    key_pos = jnp.arange(3 * block_len, dtype=jnp.int32)
    own_part = (key_pos[None, :] < block_len) & (key_pos[None, :] <= token_pos[:, None])
    pair_slot = jnp.clip(key_pos // block_len - 1, 0, 1)
    far_part = (key_pos >= block_len) & (live_pair[pair_slot] > 0)
    return own_part | far_part[None, :]


def attend_block(query_block, key_sets, value_sets, allowed):
    head_dim = key_sets.shape[1]
    flat_queries = query_block.reshape(-1, head_dim)
    scores = jnp.dot(flat_queries, key_sets.T, preferred_element_type=jnp.float32) * head_dim ** (
        -0.5
    )
    scores = jnp.where(allowed, scores, -jnp.inf)
    row_top = jnp.max(scores, axis=1, keepdims=True)
    weights = jnp.exp(scores - row_top)
    row_total = jnp.sum(weights, axis=1, keepdims=True)
    mixed = (
        jnp.dot(weights.astype(jnp.bfloat16), value_sets, preferred_element_type=jnp.float32)
        / row_total
    )
    return mixed.astype(jnp.bfloat16).reshape(query_block.shape)


def body(queries, key_vectors, value_vectors, chosen):
    blocks_here, quarter, row_width = queries.shape
    head_dim = key_vectors.shape[2]
    head_count = row_width // head_dim
    groups = lax.axis_size(("gx", "gy"))
    quarter_index = lax.axis_index("gz")
    entries = chosen.reshape(-1)
    entry_count = entries.shape[0]
    live_entry = entries >= 0
    owner_group = jnp.where(live_entry, entries // blocks_here, -1)
    local_block = jnp.where(live_entry, entries % blocks_here, 0)
    entry_ids = jnp.arange(entry_count, dtype=jnp.int32)
    same_owner = (owner_group[:, None] == owner_group[None, :]) & live_entry[None, :]
    slot_rank = jnp.sum(same_owner & (entry_ids[None, :] < entry_ids[:, None]), axis=1)
    group_ids = jnp.arange(groups, dtype=jnp.int32)
    slot_ids = jnp.arange(CAP, dtype=jnp.int32)
    hits = (owner_group[:, None, None] == group_ids[None, :, None]) & (
        slot_rank[:, None, None] == slot_ids[None, None, :]
    )
    want_table = jnp.sum(jnp.where(hits, local_block[:, None, None] + 1, 0), axis=0)
    requests = lax.all_to_all(want_table, ("gx", "gy"), split_axis=0, concat_axis=0, tiled=True)
    paired = jnp.concatenate([key_vectors, value_vectors], axis=2)
    wanted = jnp.maximum(requests - 1, 0).reshape(-1)
    outgoing = jnp.take(paired, wanted, axis=0).reshape(groups, CAP, quarter, 2 * head_dim)
    incoming = lax.all_to_all(outgoing, ("gx", "gy"), split_axis=0, concat_axis=0, tiled=True)
    incoming = incoming.reshape(groups * CAP, quarter, 2 * head_dim)
    flat_slot = jnp.maximum(owner_group, 0) * CAP + jnp.minimum(slot_rank, CAP - 1)
    fetched = jnp.take(incoming, flat_slot, axis=0)
    fetched_full, own_blocks = (
        lax.all_gather(fetched, "gz", axis=1, tiled=True),
        lax.all_gather(paired, "gz", axis=1, tiled=True),
    )
    block_len = fetched_full.shape[1]
    pair_blocks = fetched_full.reshape(blocks_here, 2, block_len, 2 * head_dim)
    live_pairs = live_entry.astype(jnp.int32).reshape(blocks_here, 2)

    def one_block(operands):
        query_block, own_pair, far_pair, live_pair = operands
        key_sets = jnp.concatenate(
            [own_pair[:, :head_dim], far_pair[0, :, :head_dim], far_pair[1, :, :head_dim]], axis=0
        )
        value_sets = jnp.concatenate(
            [own_pair[:, head_dim:], far_pair[0, :, head_dim:], far_pair[1, :, head_dim:]], axis=0
        )
        allowed = allowed_mask(quarter_index * quarter, quarter, head_count, block_len, live_pair)
        return attend_block(query_block, key_sets, value_sets, allowed)

    return lax.map(one_block, (queries, own_blocks, pair_blocks, live_pairs))


def solution(mesh):
    placed = (
        P(("gx", "gy"), "gz", None),
        P(("gx", "gy"), "gz", None),
        P(("gx", "gy"), "gz", None),
        P(("gx", "gy"), None),
    )
    return jax.shard_map(
        body, mesh=mesh, in_specs=placed, out_specs=P(("gx", "gy"), "gz", None), check_vma=False
    )
```

profile of v0, /device:TPU:73, one launch (start us, length us, event | category | flops | bytes accessed | tf_op | source)
XLA Modules:
  0.0 302.3 jit_solution(10418847764903100468)
XLA Ops:
  6.5 1.1 constant_dynamic-update-slice_fusion.2
  7.7 1.2 constant_dynamic-update-slice_fusion.1
  11.1 12.7 %all_to_all.14 = s32[32,1,1]{2,1,0:T(1,128)S(1)} all-to-all(s32[32,1,1]{2,1,0:T(1,128)S(1)} %copy.16), channel_id=1, replica_groups=mesh['gx'=4,'gy'=8,'gz'=4] {'gx','gy'}, dimensions={0} | all-to-all | bytes 256 | tf_op jit(solution)/shard_map/all_to_all | solution.py:55
  24.5 4.0 %gather_fusion = bf16[32,256,256]{2,1,0:T(8,128)(2,1)} fusion(bf16[8,256,256]{2,1,0:T(8,128)(2,1)} %copy-done, s32[1024]{0:T(1024)S(1)} %pad_clamp_fusion.1), kind=kCustom, calls=%fused_computation | custom fusion | bytes 8388736 | tf_op jit(solution)/shard_map/jit(_take)/gather | solution.py:58
  29.2 4.7 %bitcast_select_fusion = bf16[32,1,256,256]{3,2,1,0:T(8,128)(2,1)} fusion(bf16[32,256,256]{2,1,0:T(8,128)(2,1)} %gather_fusion, pred[32]{0:T(512)(128)(4,1)S(1)} %compare_reduce_fusion.1), kind=kLoop, calls=%fused_computation.54 | loop fusion | flops 2097152 | bytes 8388640 | tf_op jit(solution)/shard_map/jit(_take)/select_n | solution.py:58
  33.9 7.1 %all-to-all-start.1 = ((bf16[32,1,256,256]{3,2,1,0:T(8,128)(2,1)}), bf16[32,1,256,256]{3,2,1,0:T(8,128)(2,1)}, u32[]{:S(2)}, u32[]{:S(2)}) async-start(bf16[32,1,256,256]{3,2,1,0:T(8,128)(2,1)} %bitcast_select_fusion), calls=%async_computation.1 | async-start | bytes 8388608 | tf_op jit(solution)/shard_map/all_to_all | solution.py:59
  41.3 50.2 %all-to-all-done.1 = bf16[32,1,256,256]{3,2,1,0:T(8,128)(2,1)} async-done(((bf16[32,1,256,256]{3,2,1,0:T(8,128)(2,1)}), bf16[32,1,256,256]{3,2,1,0:T(8,128)(2,1)}, u32[]{:S(2)}, u32[]{:S(2)}) %all-to-all-start.1) | async-done | bytes 4194336 | tf_op jit(solution)/shard_map/all_to_all | solution.py:59
  91.5 2.9 gather_fusion.1
  94.3 1.6 broadcast_select_fusion
  96.1 82.6 %all-gather.5.cloned.1.call-done = bf16[16,1024,256]{2,1,0:T(8,128)(2,1)} async-done(((bf16[16,256,256]{2,1,0:T(8,128)(2,1)}), bf16[16,1024,256]{2,1,0:T(8,128)(2,1)}) %all-gather.5.cloned.1.call-update) | async-done | bytes 8388624 | tf_op jit(solution)/shard_map/all_gather | solution.py:64
  178.7 116.7 %while.13 = (s32[]{:T(128)}, bf16[8,256,512]{2,1,0:T(8,128)(2,1)}, s32[]{:T(128)}, s32[8,2]{0,1:T(2,128)S(1)}, bf16[8,256,512]{2,1,0:T(8,128)(2,1)}, /*index=5*/...) while((s32[]{:T(128)}, bf16[8,256,512]{2,1,0:T(8,128)(2,1)}, s32[]{:T(128)}, ...), condition=%wide.region_5.6_spmd, body=%wide.region_2.5_spmd.sunk | while | flops 1647116288 | bytes 48282256 | solution.py:82
  179.3 1.3 compare_reduce_fusion.3
  180.6 1.3 dynamic-slice_bitcast_fusion.4
  182.1 1.1 dynamic-slice_bitcast_fusion.5
  183.3 1.0 constant_dynamic-slice_fusion.4
  184.4 4.1 %fusion.58 = (f32[1024]{0:T(1024)S(1)}, f32[1024,3072]{1,0:T(8,128)S(1)}) fusion(bf16[1024,128]{1,0:T(8,128)(2,1)S(1)} %reshape.508, bf16[1024,128]{1,0:T(8,128)(2,1)S(1)} %get-tuple-element.211, bf16[1024,128]{1,0:T(8,128)(2,1)S(1)} %get-tuple-element.212, bf16[1024,128]{1,0:T(8,128)(2,1)S(1)} %get-tuple-element.213, ...), kind=kOutput, calls=%fused_computation.92.clone.1 | convolution fusion | flops 826539008 | bytes 13645824 | tf_op jit(solution)/shard_map/while/body/eval_jaxpr/dot_general | solution.py:21
  188.5 1.9 fusion.59
  190.3 2.0 fusion.60
  193.9 1.3 compare_reduce_fusion.3
  195.2 1.3 dynamic-slice_bitcast_fusion.4
  196.7 1.1 dynamic-slice_bitcast_fusion.5
  197.9 1.0 constant_dynamic-slice_fusion.4
  199.0 4.1 %fusion.58 = (f32[1024]{0:T(1024)S(1)}, f32[1024,3072]{1,0:T(8,128)S(1)}) fusion(bf16[1024,128]{1,0:T(8,128)(2,1)S(1)} %reshape.508, bf16[1024,128]{1,0:T(8,128)(2,1)S(1)} %get-tuple-element.211, bf16[1024,128]{1,0:T(8,128)(2,1)S(1)} %get-tuple-element.212, bf16[1024,128]{1,0:T(8,128)(2,1)S(1)} %get-tuple-element.213, ...), kind=kOutput, calls=%fused_computation.92.clone.1 | convolution fusion | flops 826539008 | bytes 13645824 | tf_op jit(solution)/shard_map/while/body/eval_jaxpr/dot_general | solution.py:21
  203.1 1.9 fusion.59
  204.9 2.0 fusion.60
  208.5 1.3 compare_reduce_fusion.3
  209.8 1.3 dynamic-slice_bitcast_fusion.4
  211.3 1.1 dynamic-slice_bitcast_fusion.5
  212.5 1.0 constant_dynamic-slice_fusion.4
  213.6 4.1 %fusion.58 = (f32[1024]{0:T(1024)S(1)}, f32[1024,3072]{1,0:T(8,128)S(1)}) fusion(bf16[1024,128]{1,0:T(8,128)(2,1)S(1)} %reshape.508, bf16[1024,128]{1,0:T(8,128)(2,1)S(1)} %get-tuple-element.211, bf16[1024,128]{1,0:T(8,128)(2,1)S(1)} %get-tuple-element.212, bf16[1024,128]{1,0:T(8,128)(2,1)S(1)} %get-tuple-element.213, ...), kind=kOutput, calls=%fused_computation.92.clone.1 | convolution fusion | flops 826539008 | bytes 13645824 | tf_op jit(solution)/shard_map/while/body/eval_jaxpr/dot_general | solution.py:21
  217.7 1.9 fusion.59
  219.5 2.0 fusion.60
  223.1 1.3 compare_reduce_fusion.3
  224.4 1.3 dynamic-slice_bitcast_fusion.4
  225.9 1.1 dynamic-slice_bitcast_fusion.5
  227.0 1.0 constant_dynamic-slice_fusion.4
  228.2 4.1 %fusion.58 = (f32[1024]{0:T(1024)S(1)}, f32[1024,3072]{1,0:T(8,128)S(1)}) fusion(bf16[1024,128]{1,0:T(8,128)(2,1)S(1)} %reshape.508, bf16[1024,128]{1,0:T(8,128)(2,1)S(1)} %get-tuple-element.211, bf16[1024,128]{1,0:T(8,128)(2,1)S(1)} %get-tuple-element.212, bf16[1024,128]{1,0:T(8,128)(2,1)S(1)} %get-tuple-element.213, ...), kind=kOutput, calls=%fused_computation.92.clone.1 | convolution fusion | flops 826539008 | bytes 13645824 | tf_op jit(solution)/shard_map/while/body/eval_jaxpr/dot_general | solution.py:21
  232.3 1.9 fusion.59
  234.1 2.0 fusion.60
  237.7 1.3 compare_reduce_fusion.3
  239.0 1.3 dynamic-slice_bitcast_fusion.4
  240.5 1.1 dynamic-slice_bitcast_fusion.5
  241.6 1.0 constant_dynamic-slice_fusion.4
  242.8 4.1 %fusion.58 = (f32[1024]{0:T(1024)S(1)}, f32[1024,3072]{1,0:T(8,128)S(1)}) fusion(bf16[1024,128]{1,0:T(8,128)(2,1)S(1)} %reshape.508, bf16[1024,128]{1,0:T(8,128)(2,1)S(1)} %get-tuple-element.211, bf16[1024,128]{1,0:T(8,128)(2,1)S(1)} %get-tuple-element.212, bf16[1024,128]{1,0:T(8,128)(2,1)S(1)} %get-tuple-element.213, ...), kind=kOutput, calls=%fused_computation.92.clone.1 | convolution fusion | flops 826539008 | bytes 13645824 | tf_op jit(solution)/shard_map/while/body/eval_jaxpr/dot_general | solution.py:21
  246.9 1.9 fusion.59
  248.7 2.0 fusion.60
  252.3 1.3 compare_reduce_fusion.3
  253.6 1.3 dynamic-slice_bitcast_fusion.4
  255.1 1.1 dynamic-slice_bitcast_fusion.5
  257.4 4.1 %fusion.58 = (f32[1024]{0:T(1024)S(1)}, f32[1024,3072]{1,0:T(8,128)S(1)}) fusion(bf16[1024,128]{1,0:T(8,128)(2,1)S(1)} %reshape.508, bf16[1024,128]{1,0:T(8,128)(2,1)S(1)} %get-tuple-element.211, bf16[1024,128]{1,0:T(8,128)(2,1)S(1)} %get-tuple-element.212, bf16[1024,128]{1,0:T(8,128)(2,1)S(1)} %get-tuple-element.213, ...), kind=kOutput, calls=%fused_computation.92.clone.1 | convolution fusion | flops 826539008 | bytes 13645824 | tf_op jit(solution)/shard_map/while/body/eval_jaxpr/dot_general | solution.py:21
  261.5 1.9 fusion.59
  263.3 2.0 fusion.60
  266.9 1.3 compare_reduce_fusion.3
  268.2 1.3 dynamic-slice_bitcast_fusion.4
  269.7 1.1 dynamic-slice_bitcast_fusion.5
  272.0 4.1 %fusion.58 = (f32[1024]{0:T(1024)S(1)}, f32[1024,3072]{1,0:T(8,128)S(1)}) fusion(bf16[1024,128]{1,0:T(8,128)(2,1)S(1)} %reshape.508, bf16[1024,128]{1,0:T(8,128)(2,1)S(1)} %get-tuple-element.211, bf16[1024,128]{1,0:T(8,128)(2,1)S(1)} %get-tuple-element.212, bf16[1024,128]{1,0:T(8,128)(2,1)S(1)} %get-tuple-element.213, ...), kind=kOutput, calls=%fused_computation.92.clone.1 | convolution fusion | flops 826539008 | bytes 13645824 | tf_op jit(solution)/shard_map/while/body/eval_jaxpr/dot_general | solution.py:21
  276.1 1.9 fusion.59
  277.9 2.0 fusion.60
  281.5 1.3 compare_reduce_fusion.3
  282.8 1.3 dynamic-slice_bitcast_fusion.4
  284.3 1.1 dynamic-slice_bitcast_fusion.5
  286.6 4.1 %fusion.58 = (f32[1024]{0:T(1024)S(1)}, f32[1024,3072]{1,0:T(8,128)S(1)}) fusion(bf16[1024,128]{1,0:T(8,128)(2,1)S(1)} %reshape.508, bf16[1024,128]{1,0:T(8,128)(2,1)S(1)} %get-tuple-element.211, bf16[1024,128]{1,0:T(8,128)(2,1)S(1)} %get-tuple-element.212, bf16[1024,128]{1,0:T(8,128)(2,1)S(1)} %get-tuple-element.213, ...), kind=kOutput, calls=%fused_computation.92.clone.1 | convolution fusion | flops 826539008 | bytes 13645824 | tf_op jit(solution)/shard_map/while/body/eval_jaxpr/dot_general | solution.py:21
  290.7 1.9 fusion.59
  292.5 2.0 fusion.60
  (100 shorter events, 22.4 us)
Async XLA Ops:
  6.5 89.5 %all-gather.3.cloned.1.call-start = ((), (), s32[]{:S(2)}) async-start(), calls=%async_computation.2 | async-start | bytes 5242880 | tf_op jit(solution)/shard_map/all_gather | solution.py:65
  8.8 1.0 copy-start
  33.9 57.6 %all-to-all-start.1 = ((bf16[32,1,256,256]{3,2,1,0:T(8,128)(2,1)}), bf16[32,1,256,256]{3,2,1,0:T(8,128)(2,1)}, u32[]{:S(2)}, u32[]{:S(2)}) async-start(bf16[32,1,256,256]{3,2,1,0:T(8,128)(2,1)} %bitcast_select_fusion), calls=%async_computation.1 | async-start | bytes 8388608 | tf_op jit(solution)/shard_map/all_to_all | solution.py:59
  40.9 137.7 %all-gather.5.cloned.1.call-start = ((), (), s32[]{:S(2)}) async-start(), calls=%async_computation.3 | async-start | bytes 10485760 | tf_op jit(solution)/shard_map/all_gather | solution.py:64
  94.3 1.7 copy-start.1
Sparse Core Ops, SparseCore 0:
  10.0 48.9 all-gather.2
  96.1 82.5 all-gather.4
where the time goes:
time: 306 us; the launch traced here: 302 us
  waiting for transfers between devices  133 us (43%)
  local copies, waits for them, and re-layouts  53.4 us (17%)
  matrix products  48.6 us (16%)
  other arithmetic  33.4 us (11%)
  between operations  13.5 us (4%)
  blocking collectives  12.7 us (4%)
  starting transfers between devices  7.29 us (2%)
    all_gather x1, waiting for transfers between devices, body(): lax.all_gather(fetched, 'gz', axis=1, tiled=True)  82.6 us
    all_to_all x1, waiting for transfers between devices, body(): lax.all_to_all(outgoing, ('gx', 'gy'), split_axis=0, concat_axis=0, tiled...  50.2 us
    dot_general x8, matrix products, attend_block(): jnp.dot(flat_queries, key_sets.T, preferred_element_type=jnp.float32)  32.5 us
    squeeze x16, local copies, waits for them, and re-layouts, body(): return lax.map(one_block, (queries, own_blocks, pair_blocks, live_pairs))  19.1 us
    dot_general x8, matrix products, attend_block(): jnp.dot(weights.astype(jnp.bfloat16), value_sets, preferred_element_type=...  16.1 us
    reduce_sum x8, other arithmetic, attend_block(): row_total = jnp.sum(weights, axis=1, keepdims=True)  14.8 us
    all_to_all x1, blocking collectives, body(): lax.all_to_all(want_table, ('gx', 'gy'), split_axis=0, concat_axis=0, til...  12.7 us
    gt x8, other arithmetic, allowed_mask(): far_part = (key_pos >= block_len) & (live_pair[pair_slot] > 0)  10.5 us
  transfers between devices with their start and end apart: 3, of which 2 were waited for; matrix products, arithmetic and copies ran while one was open for 5% of the time, Pallas kernels for 0%

commit v1 on v0

v1 whole, which is shorter than its diff:
```python
import functools

import jax
import jax.numpy as jnp
from jax import lax
from jax.experimental import pallas as pl
from jax.experimental.pallas import tpu as pltpu
from jax.sharding import PartitionSpec as P

MESH = pl.DeviceIdType.MESH
STAGES = (64, 64, 64, 64)
AHEAD = 2
PAIR = 2
NEG = -1e30
LOG2E = 1.4426950408889634


def kernel(dims, ch, q_hbm, k_hbm, v_hbm, out_hbm, *scratch):
    NX, NY, NZ, HEADS, DH, QT, ROWS = dims
    NG = NX * NY
    S = len(STAGES)
    STARTS = [sum(STAGES[:s]) for s in range(S)]
    BLOCKS = NZ * ROWS
    qb, okv, want, rqv, rqs, m_s, l_s, acc, obuf = scratch[:9]
    kv_sem, self_sem, y_send, y_recv, w_send, w_recv, rq_sem = scratch[9:16]
    a_send, a_recv, f_send, f_recv, o_send, o_recv = scratch[16:22]
    stg, recv, kvb, sel, far = (scratch[22 + S * n : 22 + S * (n + 1)] for n in range(5))

    gx, gy, gz = lax.axis_index("gx"), lax.axis_index("gy"), lax.axis_index("gz")
    g = gx * NY + gy
    xx, cc = gy // 2, lax.rem(gy, 2)
    NXX = NY // 2

    def plane(t):
        return (t // NY, lax.rem(t, NY), gz)

    def line(d):
        return lax.rem(gz + d, NZ)

    loads = []
    for s in range(S):
        for c, src in enumerate((k_hbm, v_hbm)):
            loads.append(
                pltpu.make_async_copy(
                    src.at[:, pl.ds(STARTS[s], STAGES[s])], kvb[s].at[:, c], kv_sem.at[2 * s + c]
                )
            )
    mine = pl.ds(ROWS * gz, ROWS)
    selfs = [
        pltpu.make_async_copy(k_hbm.at[mine], okv.at[:, gz, 0], self_sem.at[0]),
        pltpu.make_async_copy(v_hbm.at[mine], okv.at[:, gz, 1], self_sem.at[1]),
        pltpu.make_async_copy(q_hbm.at[mine], qb.at[:, gz], self_sem.at[2]),
    ]
    for cp in loads + selfs:
        cp.start()

    rqv[...] = jnp.zeros((NG, 1, 128), jnp.int32)

    bar = pltpu.get_barrier_semaphore()

    @pl.loop(1, NG)
    def _(s):
        pl.semaphore_signal(
            bar, 1, device_id=plane(lax.rem(g + s, NG)), device_id_type=MESH
        )

    for d in range(1, NZ):
        pl.semaphore_signal(bar, 1, device_id=(gx, gy, line(d)), device_id_type=MESH)

    owner_row = lax.broadcasted_iota(jnp.int32, (NG, 1, 128), 0)
    table = jnp.zeros((NG, 1, 128), jnp.int32)
    for b in range(BLOCKS):
        for j in range(2):
            e = ch[j, b]
            live = e >= 0
            o = jnp.where(live, lax.shift_right_logical(e, 3), -1)
            table = jnp.where(owner_row == o, lax.bitwise_and(e, 7) + 1, table)
    want[...] = table
    pl.semaphore_wait(bar, NG - 1 + NZ - 1)

    def ask(t, slot):
        return pltpu.make_async_remote_copy(
            src_ref=want.at[t], dst_ref=rqv.at[slot], send_sem=w_send.at[t],
            recv_sem=w_recv.at[slot], device_id=plane(t), device_id_type=MESH,
        )

    def sends_to(t):
        return (t > g) & (t >= 2)

    def gets_from(t):
        return (t < g) & (g >= 2)

    @pl.loop(0, NG)
    def _(t):
        @pl.when(gets_from(t))
        def _():
            ask(t, g).start()

    def ycopies(r, d):
        row, z, src_z = ROWS * line(d) + r, line(d), gz
        out = []
        for n, (src, dst) in enumerate(
            (
                (k_hbm.at[row], okv.at[r, src_z, 0]),
                (v_hbm.at[row], okv.at[r, src_z, 1]),
                (q_hbm.at[row], qb.at[r, src_z]),
            )
        ):
            out.append(
                pltpu.make_async_remote_copy(
                    src_ref=src, dst_ref=dst, send_sem=y_send.at[r, d - 1, n],
                    recv_sem=y_recv.at[r, d - 1, n], device_id=(gx, gy, z), device_id_type=MESH,
                )
            )
        return out

    DORDER = (1, 3, 2)
    for r in range(ROWS):
        for d in DORDER:
            for cp in ycopies(r, d):
                cp.start()

    for cp in loads:
        cp.wait()

    @pl.loop(0, NG)
    def _(t):
        @pl.when(sends_to(t))
        def _():
            ask(t, t).wait_recv()

        @pl.when(gets_from(t))
        def _():
            ask(t, g).wait_send()

    rq = pltpu.make_async_copy(rqv, rqs, rq_sem)
    rq.start()
    rq.wait()

    def give(s, t, slot):
        return pltpu.make_async_remote_copy(
            src_ref=stg[s].at[t], dst_ref=recv[s].at[slot], send_sem=a_send.at[s, t],
            recv_sem=a_recv.at[s, slot], device_id=plane(t), device_id_type=MESH,
        )

    def shifted(dz, dx, dc):
        return (
            lax.rem(gx + dz, NX) * NY + lax.rem(xx + dx, NXX) * 2 + lax.rem(cc + dc, 2)
        )

    def stage(s):
        @pl.loop(0, NG)
        def _(t):
            @pl.when(sends_to(t))
            def _():
                idx = jnp.maximum(rqs[t, 0, 0] - 1, 0)
                stg[s][t] = kvb[s][idx]

        recv[s][g] = kvb[s][0]

    def fire(s):
        def one(t):
            @pl.when(sends_to(t))
            def _():
                give(s, t, g).start()

        @pl.loop(0, 8)
        def _(i):
            one(shifted(i // 2, 2, lax.rem(i, 2)))

        @pl.loop(0, 16)
        def _(i):
            one(shifted(i // 4, 1 + 2 * lax.rem(i // 2, 2), lax.rem(i, 2)))

        @pl.loop(1, 8)
        def _(i):
            one(shifted(i // 2, 0, lax.rem(i, 2)))

    for s in range(S):
        stage(s)
        if s < AHEAD:
            fire(s)

    c2 = DH ** -0.5 * LOG2E

    def heads_of(r, qq, h):
        return qb[r, qq, :, h * DH : (h + 1) * DH]

    def scores_of(r, qq, h, keys):
        return lax.dot_general(
            heads_of(r, qq, h), keys, (((1,), (1,)), ((), ())),
            preferred_element_type=jnp.float32,
        )

    def weigh(p, values):
        ones = jnp.ones(values.shape, jnp.bfloat16)
        both = jnp.dot(
            p.astype(jnp.bfloat16), jnp.concatenate([values, ones], axis=1),
            preferred_element_type=jnp.float32,
        )
        return both[:, :DH], both[:, DH:]

    tok = lax.broadcasted_iota(jnp.int32, (QT, QT), 0)
    key_pos = lax.broadcasted_iota(jnp.int32, (QT, QT), 1)
    diag = key_pos <= tok

    def wide(x, n):
        return jnp.concatenate([x] * (n // DH), axis=1) if n > DH else x

    def pipeline(items):
        ready = items[0][0]()
        for n, (_, finish) in enumerate(items):
            ahead = items[n + 1][0]() if n + 1 < len(items) else None
            finish(ready)
            ready = ahead

    def peak(sc):
        return jnp.broadcast_to(jnp.max(sc, axis=1, keepdims=True), (QT, DH))

    def own_item(r, qq, h):
        n = qq + 1

        def first():
            return scores_of(r, qq, h, okv[r, 0:n, 0].reshape(n * QT, DH))

        def finish(sc):
            last = jnp.where(diag, sc[:, qq * QT :], NEG)
            sc = jnp.concatenate([sc[:, : qq * QT], last], axis=1) if qq else last
            top = peak(sc)
            p = jnp.exp2(sc * c2 - wide(top * c2, n * QT))
            pv, tot = weigh(p, okv[r, 0:n, 1].reshape(n * QT, DH))
            m_s[r, qq, h] = top
            l_s[r, qq, h] = tot
            acc[r, qq, h] = pv

        return first, finish

    def own(r):
        pipeline([own_item(r, qq, h) for qq in range(NZ) for h in range(HEADS)])

    def far_item(s, r, qq, h, live, last):
        n = 2 * NZ * STAGES[s]

        def first():
            return scores_of(r, qq, h, far[s][r, :, :, 0].reshape(n, DH))

        def finish(sc):
            old = m_s[r, qq, h]
            new = jnp.where(live, jnp.maximum(old, peak(sc)), old)
            base = jnp.where(live, new * c2, -NEG)
            p = jnp.exp2(sc * c2 - wide(base, n))
            fade = jnp.exp2((old - new) * c2)
            pv, tot = weigh(p, far[s][r, :, :, 1].reshape(n, DH))
            a_new = acc[r, qq, h] * fade + pv
            l_new = l_s[r, qq, h] * fade + tot
            if last:
                obuf[r, qq, :, h * DH : (h + 1) * DH] = (a_new / l_new).astype(jnp.bfloat16)
            else:
                m_s[r, qq, h] = new
                acc[r, qq, h] = a_new
                l_s[r, qq, h] = l_new

        return first, finish

    def extend(s, r, qqs, last):
        live = ch[0, ROWS * gz + r] >= 0
        pipeline([far_item(s, r, qq, h, live, last) for qq in qqs for h in range(HEADS)])

    def fcopy(s, r, d):
        return pltpu.make_async_remote_copy(
            src_ref=sel[s].at[r, d - 1], dst_ref=far[s].at[r, gz],
            send_sem=f_send.at[s, r, d - 1], recv_sem=f_recv.at[s, r, d - 1],
            device_id=(gx, gy, line(d)), device_id_type=MESH,
        )

    def forward(s):
        @pl.loop(0, NG)
        def _(t):
            @pl.when(gets_from(t))
            def _():
                give(s, t, t).wait_recv()

        if s + AHEAD < S:
            fire(s + AHEAD)

        for r in range(ROWS):
            for d in DORDER + (NZ,):
                for j in range(2):
                    e = ch[j, ROWS * line(d) + r]
                    o = jnp.where(e >= 0, lax.shift_right_logical(e, 3), g)
                    val = recv[s][o]
                    if d < NZ:
                        sel[s][r, d - 1, j] = val
                    else:
                        far[s][r, gz, j] = val
            for d in DORDER:
                fcopy(s, r, d).start()

    def wait_own(r):
        for d in DORDER:
            for cp in ycopies(r, d):
                cp.wait_recv()

    def wait_far(s, r):
        for d in DORDER:
            fcopy(s, r, d).wait_recv()

    for cp in selfs:
        cp.wait()
    wait_own(0)
    own(0)
    forward(0)
    wait_own(1)
    own(1)
    if S > 1:
        forward(1)
    for s in range(S - 1):
        for r in range(ROWS):
            wait_far(s, r)

            @pl.loop(0, NZ // PAIR)
            def _(i, s=s, r=r):
                extend(s, r, [PAIR * i + n for n in range(PAIR)], False)

        if s + 2 < S:
            forward(s + 2)

    def ocopy(r, d):
        return pltpu.make_async_remote_copy(
            src_ref=obuf.at[r, line(d)], dst_ref=out_hbm.at[ROWS * gz + r],
            send_sem=o_send.at[r, d - 1], recv_sem=o_recv.at[r, d - 1],
            device_id=(gx, gy, line(d)), device_id_type=MESH,
        )

    def olocal(r):
        return pltpu.make_async_copy(
            obuf.at[r, gz], out_hbm.at[ROWS * gz + r], o_send.at[r, NZ - 1]
        )

    for r in range(ROWS):
        wait_far(S - 1, r)

        @pl.loop(1, NZ + 1)
        def _(d, r=r):
            extend(S - 1, r, [lax.rem(gz + d, NZ)], True)

            @pl.when(d >= 2)
            def _():
                ocopy(r, d - 1).start()

        olocal(r).start()

    for r in range(ROWS):
        for d in range(1, NZ):
            for cp in ycopies(r, d):
                cp.wait_send()
            for s in range(S):
                fcopy(s, r, d).wait_send()
    for s in range(S):

        @pl.loop(0, NG)
        def _(t, s=s):
            @pl.when(sends_to(t))
            def _():
                give(s, t, g).wait_send()

    for r in range(ROWS):
        for d in range(1, NZ):
            ocopy(r, d).wait()
        olocal(r).wait()


def body(queries, key_vectors, value_vectors, chosen):
    blocks, quarter, width = queries.shape
    dh = key_vectors.shape[2]
    heads = width // dh
    nx, ny, nz = (lax.axis_size(a) for a in ("gx", "gy", "gz"))
    rows = blocks // nz
    ng = nx * ny
    s = len(STAGES)
    bf, f32, i32 = jnp.bfloat16, jnp.float32, jnp.int32
    dma = pltpu.SemaphoreType.DMA
    scratch = [
        pltpu.VMEM((rows, nz, quarter, width), bf),
        pltpu.VMEM((rows, nz, 2, quarter, dh), bf),
        pltpu.VMEM((ng, 1, 128), i32),
        pltpu.VMEM((ng, 1, 128), i32),
        pltpu.SMEM((ng, 1, 128), i32),
        pltpu.VMEM((rows, nz, heads, quarter, dh), f32),
        pltpu.VMEM((rows, nz, heads, quarter, dh), f32),
        pltpu.VMEM((rows, nz, heads, quarter, dh), f32),
        pltpu.VMEM((rows, nz, quarter, width), bf),
        dma((2 * s,)),
        dma((3,)),
        dma((rows, nz - 1, 3)),
        dma((rows, nz - 1, 3)),
        dma((ng,)),
        dma((ng,)),
        dma,
        dma((s, ng)),
        dma((s, ng)),
        dma((s, rows, nz - 1)),
        dma((s, rows, nz - 1)),
        dma((rows, nz)),
        dma((rows, nz)),
    ]
    for lead in ((ng,), (ng,), (blocks,), (rows, nz - 1, 2), (rows, nz, 2)):
        scratch += [pltpu.VMEM(lead + (2, t, dh), bf) for t in STAGES]
    return pl.pallas_call(
        functools.partial(kernel, (nx, ny, nz, heads, dh, quarter, rows)),
        out_shape=jax.ShapeDtypeStruct(queries.shape, bf),
        in_specs=[pl.BlockSpec(memory_space=pltpu.SMEM)]
        + [pl.BlockSpec(memory_space=pl.ANY)] * 3,
        out_specs=pl.BlockSpec(memory_space=pl.ANY),
        scratch_shapes=scratch,
        compiler_params=pltpu.CompilerParams(
            collective_id=0, has_side_effects=True, vmem_limit_bytes=60 * 1024 * 1024
        ),
    )(chosen.T, queries, key_vectors, value_vectors)


def solution(mesh):
    placed = (
        P(("gx", "gy"), "gz", None),
        P(("gx", "gy"), "gz", None),
        P(("gx", "gy"), "gz", None),
        P(("gx", "gy"), None),
    )
    return jax.shard_map(
        body, mesh=mesh, in_specs=placed, out_specs=P(("gx", "gy"), "gz", None), check_vma=False
    )
```

time: 306 us -> 110 us (0.36); the launches traced: 302 us -> 110 us
  waiting for transfers between devices: 133 us -> 0 us
  Pallas kernels: 0 us -> 107 us
  local copies, waits for them, and re-layouts: 53.4 us -> 3.05 us
  matrix products: 48.6 us -> 0 us
  other arithmetic: 33.4 us -> 0 us
  between operations: 13.5 us -> 0.01 us
  blocking collectives: 12.7 us -> 0 us
  starting transfers between devices: 7.29 us -> 0 us
    pallas_call x0 -> x1, Pallas kernels: none -> 107 us  [body(): pl.pallas_call(functools.partial(kernel, (nx, ny, nz, heads, dh, quarter,...]
    all_gather x2 -> x0, waiting for transfers between devices: 82.6 us -> none  [the longest x1 82.6 us: body(): lax.all_gather(fetched, 'gz', axis=1, tiled=True)]
    all_to_all x1 -> x0, waiting for transfers between devices: 50.2 us -> none  [body(): lax.all_to_all(outgoing, ('gx', 'gy'), split_axis=0, concat_axis=0, tiled...]
    dot_general x16 -> x0, matrix products: 48.6 us -> none  [the longest x8 32.5 us: attend_block(): jnp.dot(flat_queries, key_sets.T, preferred_element_type=jnp.float32)]
    squeeze x24 -> x0, local copies, waits for them, and re-layouts: 20.5 us -> none  [the longest x16 19.1 us: body(): return lax.map(one_block, (queries, own_blocks, pair_blocks, live_pairs))]
    reduce_sum x10 -> x0, other arithmetic: 15.1 us -> none  [the longest x8 14.8 us: attend_block(): row_total = jnp.sum(weights, axis=1, keepdims=True)]
    all_to_all x1 -> x0, blocking collectives: 12.7 us -> none  [body(): lax.all_to_all(want_table, ('gx', 'gy'), split_axis=0, concat_axis=0, til...]
    gather x10 -> x0, local copies, waits for them, and re-layouts: 11.5 us -> none  [the longest x8 4.65 us: allowed_mask(): far_part = (key_pos >= block_len) & (live_pair[pair_slot] > 0)]
  transfers between devices with their start and end apart: 3 -> 0, of which waited for: 2 -> 0; matrix products, arithmetic and copies ran while one was open for 5% -> 0% of each run, Pallas kernels for 0% -> 0%
where the time goes in v1:
time: 110 us
  Pallas kernels  107 us (97%)
  local copies, waits for them, and re-layouts  3.05 us (3%)
    pallas_call x1, Pallas kernels, body(): pl.pallas_call(functools.partial(kernel, (nx, ny, nz, heads, dh, quarter,...  107 us
    unnamed x1, local copies, waits for them, and re-layouts  3.05 us

profile of v1, /device:TPU:73, one launch (start us, length us, event | category | flops | bytes accessed | tf_op | source)
XLA Modules:
  0.0 110.1 jit_solution(13441718720903773219)
XLA Ops:
  0.0 107.1 %shard_map.46 = bf16[8,256,512]{2,1,0:T(8,128)(2,1)} custom-call(s32[2,8]{1,0:T(2,128)} %bitcast.1, bf16[8,256,512]{2,1,0:T(8,128)(2,1)} %q_hbm.1, bf16[8,256,128]{2,1,0:T(8,128)(2,1)} %k_hbm.1, bf16[8,256,128]{2,1,0:T(8,128)(2,1)} %v_hbm.1), custom_call_target="tpu_custom_call" | custom-call | tf_op jit(solution)/shard_map/pallas_call | solution.py:409
  107.1 3.0 %copy.6 = bf16[8,256,512]{2,1,0:T(8,128)(2,1)} copy(bf16[8,256,512]{2,1,0:T(8,128)(2,1)} %shard_map.46) | data formatting | bytes 4194304

commit v2 on v1

--- a/solution.py
+++ b/solution.py
@@ -15,7 +15,7 @@
 LOG2E = 1.4426950408889634
 
 
-def kernel(dims, ch, q_hbm, k_hbm, v_hbm, out_hbm, *scratch):
+def kernel(dims, ch, q_hbm, k_hbm, v_hbm, out_ref, *scratch):
     NX, NY, NZ, HEADS, DH, QT, ROWS = dims
     NG = NX * NY
     S = len(STAGES)
@@ -129,10 +129,6 @@
         def _():
             ask(t, t).wait_recv()
 
-        @pl.when(gets_from(t))
-        def _():
-            ask(t, g).wait_send()
-
     rq = pltpu.make_async_copy(rqv, rqs, rq_sem)
     rq.start()
     rq.wait()
@@ -327,14 +323,9 @@
 
     def ocopy(r, d):
         return pltpu.make_async_remote_copy(
-            src_ref=obuf.at[r, line(d)], dst_ref=out_hbm.at[ROWS * gz + r],
+            src_ref=obuf.at[r, line(d)], dst_ref=out_ref.at[ROWS * gz + r],
             send_sem=o_send.at[r, d - 1], recv_sem=o_recv.at[r, d - 1],
             device_id=(gx, gy, line(d)), device_id_type=MESH,
-        )
-
-    def olocal(r):
-        return pltpu.make_async_copy(
-            obuf.at[r, gz], out_hbm.at[ROWS * gz + r], o_send.at[r, NZ - 1]
         )
 
     for r in range(ROWS):
@@ -348,7 +339,13 @@
             def _():
                 ocopy(r, d - 1).start()
 
-        olocal(r).start()
+        out_ref[ROWS * gz + r] = obuf[r, gz]
+
+    @pl.loop(0, NG)
+    def _(t):
+        @pl.when(gets_from(t))
+        def _():
+            ask(t, g).wait_send()
 
     for r in range(ROWS):
         for d in range(1, NZ):
@@ -367,7 +364,6 @@
     for r in range(ROWS):
         for d in range(1, NZ):
             ocopy(r, d).wait()
-        olocal(r).wait()
 
 
 def body(queries, key_vectors, value_vectors, chosen):
@@ -401,20 +397,20 @@
         dma((s, ng)),
         dma((s, rows, nz - 1)),
         dma((s, rows, nz - 1)),
-        dma((rows, nz)),
-        dma((rows, nz)),
+        dma((rows, nz - 1)),
+        dma((rows, nz - 1)),
     ]
     for lead in ((ng,), (ng,), (blocks,), (rows, nz - 1, 2), (rows, nz, 2)):
         scratch += [pltpu.VMEM(lead + (2, t, dh), bf) for t in STAGES]
     return pl.pallas_call(
         functools.partial(kernel, (nx, ny, nz, heads, dh, quarter, rows)),
-        out_shape=jax.ShapeDtypeStruct(queries.shape, bf),
+        out_shape=pltpu.VMEM(queries.shape, bf),
         in_specs=[pl.BlockSpec(memory_space=pltpu.SMEM)]
-        + [pl.BlockSpec(memory_space=pl.ANY)] * 3,
-        out_specs=pl.BlockSpec(memory_space=pl.ANY),
+        + [pl.BlockSpec(memory_space=pltpu.HBM)] * 3,
+        out_specs=pl.BlockSpec(memory_space=pltpu.VMEM),
         scratch_shapes=scratch,
         compiler_params=pltpu.CompilerParams(
-            collective_id=0, has_side_effects=True, vmem_limit_bytes=60 * 1024 * 1024
+            collective_id=0, has_side_effects=True, vmem_limit_bytes=67043328 - 9 * 262144
         ),
     )(chosen.T, queries, key_vectors, value_vectors)
 

time: 110 us -> 108 us (0.982)
  local copies, waits for them, and re-layouts: 3.05 us -> 1.32 us
    unnamed x1, local copies, waits for them, and re-layouts: 3.05 us -> 1.32 us
where the time goes in v2:
time: 108 us
  Pallas kernels  107 us (99%)
  local copies, waits for them, and re-layouts  1.32 us (1%)
    pallas_call x1, Pallas kernels, body(): pl.pallas_call(functools.partial(kernel, (nx, ny, nz, heads, dh, quarter,...  107 us

profile of v2, /device:TPU:73, one launch (start us, length us, event | category | flops | bytes accessed | tf_op | source)
XLA Modules:
  0.0 108.2 jit_solution(9477992241684036233)
XLA Ops:
  0.0 106.9 %shard_map.46 = bf16[8,256,512]{2,1,0:T(8,128)(2,1)S(1)} custom-call(s32[2,8]{1,0:T(2,128)} %bitcast.1, bf16[8,256,512]{2,1,0:T(8,128)(2,1)} %q_hbm.1, bf16[8,256,128]{2,1,0:T(8,128)(2,1)} %k_hbm.1, bf16[8,256,128]{2,1,0:T(8,128)(2,1)} %v_hbm.1), custom_call_target="tpu_custom_call" | custom-call | tf_op jit(solution)/shard_map/pallas_call | solution.py:405
  106.9 1.3 %copy.6 = bf16[8,256,512]{2,1,0:T(8,128)(2,1)} copy(bf16[8,256,512]{2,1,0:T(8,128)(2,1)S(1)} %shard_map.46) | data formatting | bytes 4194304

commit v3 on v2

--- a/solution.py
+++ b/solution.py
@@ -114,7 +114,7 @@
             )
         return out
 
-    DORDER = (1, 3, 2)
+    DORDER = (2, 1, 3)
     for r in range(ROWS):
         for d in DORDER:
             for cp in ycopies(r, d):

time: 108 us -> 108 us (level)
  no operation moved by 1% of the time
where the time goes in v3:
time: 108 us
  Pallas kernels  107 us (99%)
  local copies, waits for them, and re-layouts  1.32 us (1%)
    pallas_call x1, Pallas kernels, body(): pl.pallas_call(functools.partial(kernel, (nx, ny, nz, heads, dh, quarter,...  107 us

profile of v3, /device:TPU:73, one launch (start us, length us, event | category | flops | bytes accessed | tf_op | source)
XLA Modules:
  0.0 107.9 jit_solution(3562524345888024278)
XLA Ops:
  0.0 106.6 %shard_map.46 = bf16[8,256,512]{2,1,0:T(8,128)(2,1)S(1)} custom-call(s32[2,8]{1,0:T(2,128)} %bitcast.1, bf16[8,256,512]{2,1,0:T(8,128)(2,1)} %q_hbm.1, bf16[8,256,128]{2,1,0:T(8,128)(2,1)} %k_hbm.1, bf16[8,256,128]{2,1,0:T(8,128)(2,1)} %v_hbm.1), custom_call_target="tpu_custom_call" | custom-call | tf_op jit(solution)/shard_map/pallas_call | solution.py:405
  106.6 1.3 %copy.6 = bf16[8,256,512]{2,1,0:T(8,128)(2,1)} copy(bf16[8,256,512]{2,1,0:T(8,128)(2,1)S(1)} %shard_map.46) | data formatting | bytes 4194304
